TPU v7x, 256 devices: a whole 4x4x8 slice. The times are simulated.
256 devices in a mesh: slab: 256 (over x, z, y, core).
Axes of the slice: x: 4, y: 4, z: 8, core: 2. Of those that a mesh axis runs over, the one named last changes fastest.
Arguments:
- coords: float32 [3, 524288], P(None, 'slab'), may hold values from -18 to 2048, as said below
- charges: float32 [524288], P('slab'), may hold values from -3.6 to 3.6
- radii: float32 [524288], P('slab'), may hold values from 1.2 to 2
- screens: float32 [524288], P('slab'), may hold values from 0.6 to 0.9
- tile_lists: int32 [4096, 8], P('slab'), may hold values from 0 to 79, as said below
- tile_counts: int32 [4096], P('slab'), may hold values from 1 to 8, as said below
- slab_fill: int32 [256], P('slab'), may hold values from 1921 to 2048
Outputs:
- born_radii: float32 [524288], P('slab')
- energy: float32 [524288], P('slab')
- total: float32 [], replicated
Inputs may be any that keep to these rules, and one draw needn't show every extreme that they name: `coords`: x and y lie within 18 of the fibre axis; z of atoms of slab s lies in [8 s, 8 s + 8]. `tile_lists`: entry 0 of tile g's list is its own tile, 32 + g % 16; the entries of a row are distinct; listed tiles lie in slabs that exist (the fibre does not close) and within 32 window tiles of the own tile. `tile_counts`: every slab has a tile whose count is 8.
All inputs are finite; a program needn't handle non-finite values.
Results may differ from a plain program's by a relative error of at most 0.0003.
Values sent between devices are 32-bit elements; how exact they have to be, the bound alone decides.
No kernel may reach another device: no remote copies, remote signals or barrier semaphores. Data moves between devices by JAX's collectives and lax.ppermute only.
A program may use at most 64 MiB of HBM per device.

v0:
```python
import jax
import jax.numpy as jnp
from jax import lax
from jax.sharding import Mesh
from jax.sharding import PartitionSpec as P

SLAB = ("slab_0", "slab_1", "slab_2", "slab_3")
OFFSET = 0.09
SOFTEN = 1.0
group_tiles = 4


def passed_along(value, axis, steps):
    count = lax.axis_size(axis)
    pairs = [(source, (source + steps) % count) for source in range(count)]
    return lax.ppermute(value, axis, pairs)


def by_axis(shard, axes):
    for axis in axes:
        shard = lax.psum(shard, axis)
    return shard


def pair_geometry(own_atoms, partner_atoms, list_block, count_block, first_block):
    squared = jnp.zeros((own_atoms.shape[1], 128, partner_atoms.shape[2], 128), jnp.float32)
    for component in range(3):
        offsets = own_atoms[component][:, :, None, None] - partner_atoms[component][:, None, :, :]
        squared = squared + offsets * offsets
    slot_ids = jnp.arange(partner_atoms.shape[2], dtype=jnp.int32)
    used_slot = (slot_ids[None, :] < count_block[:, None])[:, None, :, None]
    partner_mask = (
        used_slot & (partner_atoms[6] > 0.5)[:, None, :, :] & (own_atoms[6] > 0.5)[:, :, None, None]
    )
    lanes = jnp.arange(128, dtype=jnp.int32)
    own_ids = first_block[:, None] * 128 + lanes[None, :]
    partner_ids = list_block[:, :, None] * 128 + lanes[None, None, :]
    distinct = own_ids[:, :, None, None] != partner_ids[:, None, :, :]
    return (squared, partner_mask, distinct)


def born_block(own_atoms, partner_atoms, list_block, count_block, first_block):
    squared, partner_mask, distinct = pair_geometry(
        own_atoms, partner_atoms, list_block, count_block, first_block
    )
    own_live = own_atoms[6] > 0.5
    radius_own = jnp.where(own_live, own_atoms[4], 1.5)
    radius_partner = jnp.where(partner_atoms[6] > 0.5, partner_atoms[4], 1.5)[:, None, :, :]
    screen_partner = jnp.where(partner_atoms[6] > 0.5, partner_atoms[5], 0.8)[:, None, :, :]
    offset_radius = (radius_own - OFFSET)[:, :, None, None]
    scaled_radius = screen_partner * (radius_partner - OFFSET)
    distance = jnp.sqrt(squared + SOFTEN)
    upper_end = distance + scaled_radius
    lower_end = jnp.maximum(offset_radius, jnp.abs(distance - scaled_radius))
    pair_term = 0.5 * (
        1.0 / lower_end
        - 1.0 / upper_end
        + 0.25
        * (distance - scaled_radius * scaled_radius / distance)
        * (1.0 / (upper_end * upper_end) - 1.0 / (lower_end * lower_end))
        + 0.5 * jnp.log(lower_end / upper_end) / distance
    )
    pair_term = pair_term + jnp.where(
        offset_radius < scaled_radius - distance, 2.0 * (1.0 / offset_radius - 1.0 / lower_end), 0.0
    )
    counted = partner_mask & distinct & (offset_radius < upper_end)
    integral = jnp.sum(jnp.where(counted, pair_term, 0.0), axis=(2, 3))
    inner_radius = radius_own - OFFSET
    psi_value = integral * inner_radius
    bending = jnp.tanh(
        psi_value - 0.8 * psi_value * psi_value + 4.85 * psi_value * psi_value * psi_value
    )
    result = 1.0 / (1.0 / inner_radius - bending / radius_own)
    return jnp.where(own_live, result, 0.0)


def energy_block(
    own_atoms, partner_atoms, radius_own, radius_partner, list_block, count_block, first_block
):
    squared, partner_mask, distinct = pair_geometry(
        own_atoms, partner_atoms, list_block, count_block, first_block
    )
    own_live = own_atoms[6] > 0.5
    born_own = jnp.where(own_live, radius_own, 1.0)[:, :, None, None]
    born_partner = jnp.where(partner_atoms[6] > 0.5, radius_partner, 1.0)[:, None, :, :]
    product = born_own * born_partner
    screened = jnp.sqrt(squared + product * jnp.exp(-squared / (4.0 * product)))
    pair_term = jnp.where(partner_mask, partner_atoms[3][:, None, :, :] / screened, 0.0)
    result = -0.5 * own_atoms[3] * jnp.sum(pair_term, axis=(2, 3))
    return jnp.where(own_live, result, 0.0)


def tile_setup(window, lists, counts):
    width = window.shape[1]
    tiles = width // 640
    blocks = tiles // group_tiles
    tiled = window.reshape(window.shape[0], width // 128, 128)
    own_atoms = (
        tiled[:, 2 * tiles : 3 * tiles]
        .reshape(window.shape[0], blocks, group_tiles, 128)
        .transpose(1, 0, 2, 3)
    )
    list_groups = lists.reshape(blocks, group_tiles, lists.shape[1])
    count_groups = counts.reshape(blocks, group_tiles)
    first_tiles = (2 * tiles + jnp.arange(tiles, dtype=jnp.int32)).reshape(blocks, group_tiles)
    return (tiled, own_atoms, list_groups, count_groups, first_tiles)


def slab_born(window, lists, counts):
    tiled, own_atoms, list_groups, count_groups, first_tiles = tile_setup(window, lists, counts)

    def one_block(inputs):
        own_block, list_block, count_block, first_block = inputs
        partner_atoms = jnp.take(tiled, list_block, axis=1)
        return born_block(own_block, partner_atoms, list_block, count_block, first_block)

    result = lax.map(one_block, (own_atoms, list_groups, count_groups, first_tiles))
    return result.reshape(-1)


def slab_energy(window, radius_window, lists, counts):
    tiled, own_atoms, list_groups, count_groups, first_tiles = tile_setup(window, lists, counts)
    radius_tiled = radius_window.reshape(-1, 128)
    tiles = radius_tiled.shape[0] // 5
    radius_groups = radius_tiled[2 * tiles : 3 * tiles].reshape(-1, group_tiles, 128)

    def one_block(inputs):
        own_block, radius_block, list_block, count_block, first_block = inputs
        partner_atoms = jnp.take(tiled, list_block, axis=1)
        partner_radii = jnp.take(radius_tiled, list_block, axis=0)
        return energy_block(
            own_block,
            partner_atoms,
            radius_block,
            partner_radii,
            list_block,
            count_block,
            first_block,
        )

    result = lax.map(one_block, (own_atoms, radius_groups, list_groups, count_groups, first_tiles))
    return result.reshape(-1)


def window_of(values):
    nearby = [passed_along(values, SLAB, shift_by) for shift_by in (1, -1)]
    distant = [passed_along(values, SLAB, shift_by) for shift_by in (2, -2)]
    return jnp.concatenate([distant[0], nearby[0], values, nearby[1], distant[1]], axis=-1)


def shards(coords, charges, radii, screens, tile_lists, tile_counts, slab_fill):
    atom_count = coords.shape[1]
    live_flag = (jnp.arange(atom_count, dtype=jnp.int32) < slab_fill[0]).astype(jnp.float32)
    packed = jnp.concatenate(
        [coords, charges[None], radii[None], screens[None], live_flag[None]], axis=0
    )
    window = window_of(packed)
    born_radii = slab_born(window, tile_lists, tile_counts)
    radius_window = window_of(born_radii)
    energy = slab_energy(window, radius_window, tile_lists, tile_counts)
    total = by_axis(jnp.sum(energy), SLAB)
    return (born_radii, energy, total)


def solution(mesh):
    torus = Mesh(mesh.devices.reshape(4, 8, 4, 2), ("slab_0", "slab_1", "slab_2", "slab_3"))
    placed = (P(None, SLAB), P(SLAB), P(SLAB), P(SLAB), P(SLAB, None), P(SLAB), P(SLAB))
    return jax.shard_map(
        shards, mesh=torus, in_specs=placed, out_specs=(P(SLAB), P(SLAB), P()), check_vma=False
    )
```

profile of v0, /device:TPU:1, one launch (start us, length us, event | category | flops | bytes accessed | tf_op | source)
XLA Modules:
  0.0 163.9 jit_solution(10497928802857674621)
XLA Ops:
  1.3 0.8 concatenate.21
  2.1 2.2 %collective-permute-start = (f32[7,2048]{1,0:T(8,128)S(1)}, f32[7,2048]{1,0:T(8,128)S(1)}, u32[]{:S(2)}, u32[]{:S(2)}) collective-permute-start(f32[7,2048]{1,0:T(8,128)S(1)} %concatenate.21), channel_id=1, source_target_pairs={{0,2},{1,3},{2,4},{3,5},{4,6},{5,7},{6,8},{7,9},{8,10},{9,11},{10,... | collective-permute-start | bytes 172040 | tf_op jit(solution)/shard_map/ppermute | solution.py:16
  4.3 2.1 %collective-permute-start.1 = (f32[7,2048]{1,0:T(8,128)S(1)}, f32[7,2048]{1,0:T(8,128)S(1)}, u32[]{:S(2)}, u32[]{:S(2)}) collective-permute-start(f32[7,2048]{1,0:T(8,128)S(1)} %concatenate.21), channel_id=1, source_target_pairs={{0,1},{1,2},{2,3},{3,4},{4,5},{5,6},{6,7},{7,8},{8,9},{9,10},{10,1... | collective-permute-start | bytes 172040 | tf_op jit(solution)/shard_map/ppermute | solution.py:16
  6.5 7.6 %collective-permute-start.3 = (f32[7,2048]{1,0:T(8,128)S(1)}, f32[7,2048]{1,0:T(8,128)S(1)}, u32[]{:S(2)}, u32[]{:S(2)}) collective-permute-start(f32[7,2048]{1,0:T(8,128)S(1)} %concatenate.21), channel_id=1, source_target_pairs={{0,254},{1,255},{2,0},{3,1},{4,2},{5,3},{6,4},{7,5},{8,6},{9,7},{1... | collective-permute-start | bytes 172040 | tf_op jit(solution)/shard_map/ppermute | solution.py:16
  14.1 0.8 copy.25
  14.9 0.7 reshape.487
  15.7 0.3 collective-permute-done.3
  16.1 47.0 %while.23 = (s32[]{:T(128)}, f32[4,4,128]{2,1,0:T(4,128)S(1)}, f32[4,7,4,128]{3,2,1,0:T(4,128)S(1)}, s32[4,4]{1,0:T(4,128)S(1)}, s32[4,4,8]{2,1,0:T(4,128)S(1)},...) while((s32[]{:T(128)}, f32[4,4,128]{2,1,0:T(4,128)S(1)}, ...), condition=%wide.region_2.4_spmd, body=%wide.region_0.3_spmd.sunk | while | flops 23141128 | bytes 918585 | solution.py:117
  16.1 0.1 reshape.539
  16.2 0.6 gather_fusion
  16.8 0.1 select_bitcast_fusion.2
  17.1 0.1 bitcast_and_fusion.2
  17.4 10.4 %fusion.63 = f32[4,128]{1,0:T(4,128)S(1)} fusion(f32[4,128]{1,0:T(4,128)S(1)} %get-tuple-element.337, f32[4,8,128]{2,1,0:T(8,128)S(1)} %get-tuple-element.345, f32[4,8,128]{2,1,0:T(8,128)S(1)} %get-tuple-element.346, f32[4,8,128]{2,1,0:T(8,128)S(1)} %bitcast.188, f32[4,128]{1,0:T(4,128)S(1)} %get-tuple-element.348, f32[4,8,128]{2,1,0:T(8,128)S(1)} %bitcast.189, ...), kind=kLoop, calls=%fused_computation.16.clone.1 | loop fusion | flops 23068160 | bytes 117248 | tf_op jit(solution)/shard_map/while/body/eval_jaxpr/reduce_sum | solution.py:67
  27.9 0.1 reshape.539
  28.0 0.6 gather_fusion
  28.5 0.1 select_bitcast_fusion.2
  28.8 0.1 bitcast_and_fusion.2
  29.1 10.4 %fusion.63 = f32[4,128]{1,0:T(4,128)S(1)} fusion(f32[4,128]{1,0:T(4,128)S(1)} %get-tuple-element.337, f32[4,8,128]{2,1,0:T(8,128)S(1)} %get-tuple-element.345, f32[4,8,128]{2,1,0:T(8,128)S(1)} %get-tuple-element.346, f32[4,8,128]{2,1,0:T(8,128)S(1)} %bitcast.188, f32[4,128]{1,0:T(4,128)S(1)} %get-tuple-element.348, f32[4,8,128]{2,1,0:T(8,128)S(1)} %bitcast.189, ...), kind=kLoop, calls=%fused_computation.16.clone.1 | loop fusion | flops 23068160 | bytes 117248 | tf_op jit(solution)/shard_map/while/body/eval_jaxpr/reduce_sum | solution.py:67
  39.6 0.1 reshape.539
  39.7 0.6 gather_fusion
  40.3 0.1 select_bitcast_fusion.2
  40.6 0.1 bitcast_and_fusion.2
  40.9 10.4 %fusion.63 = f32[4,128]{1,0:T(4,128)S(1)} fusion(f32[4,128]{1,0:T(4,128)S(1)} %get-tuple-element.337, f32[4,8,128]{2,1,0:T(8,128)S(1)} %get-tuple-element.345, f32[4,8,128]{2,1,0:T(8,128)S(1)} %get-tuple-element.346, f32[4,8,128]{2,1,0:T(8,128)S(1)} %bitcast.188, f32[4,128]{1,0:T(4,128)S(1)} %get-tuple-element.348, f32[4,8,128]{2,1,0:T(8,128)S(1)} %bitcast.189, ...), kind=kLoop, calls=%fused_computation.16.clone.1 | loop fusion | flops 23068160 | bytes 117248 | tf_op jit(solution)/shard_map/while/body/eval_jaxpr/reduce_sum | solution.py:67
  51.4 0.1 reshape.539
  51.5 0.6 gather_fusion
  52.0 0.1 select_bitcast_fusion.2
  52.3 0.1 bitcast_and_fusion.2
  52.6 10.4 %fusion.63 = f32[4,128]{1,0:T(4,128)S(1)} fusion(f32[4,128]{1,0:T(4,128)S(1)} %get-tuple-element.337, f32[4,8,128]{2,1,0:T(8,128)S(1)} %get-tuple-element.345, f32[4,8,128]{2,1,0:T(8,128)S(1)} %get-tuple-element.346, f32[4,8,128]{2,1,0:T(8,128)S(1)} %bitcast.188, f32[4,128]{1,0:T(4,128)S(1)} %get-tuple-element.348, f32[4,8,128]{2,1,0:T(8,128)S(1)} %bitcast.189, ...), kind=kLoop, calls=%fused_computation.16.clone.1 | loop fusion | flops 23068160 | bytes 117248 | tf_op jit(solution)/shard_map/while/body/eval_jaxpr/reduce_sum | solution.py:67
  63.1 0.1 collective-permute-start.4
  63.2 1.4 collective-permute-start.5
  64.6 0.8 collective-permute-start.6
  65.4 7.4 %collective-permute-start.7 = (f32[2048]{0:T(1024)S(1)}, f32[2048]{0:T(1024)S(1)}, u32[]{:S(2)}, u32[]{:S(2)}) collective-permute-start(f32[2048]{0:T(1024)S(1)} %bitcast.195), channel_id=1, source_target_pairs={{0,254},{1,255},{2,0},{3,1},{4,2},{5,3},{6,4},{7,5},{8,6},{9,7},{1... | collective-permute-start | bytes 24584 | tf_op jit(solution)/shard_map/ppermute | solution.py:16
  72.8 0.7 collective-permute-done.7
  73.6 44.1 %while.24 = (s32[]{:T(128)}, f32[4,4,128]{2,1,0:T(4,128)S(1)}, f32[4,7,4,128]{3,2,1,0:T(4,128)S(1)}, s32[4,4]{1,0:T(4,128)S(1)}, s32[4,4,8]{2,1,0:T(4,128)S(1)},...) while((s32[]{:T(128)}, f32[4,4,128]{2,1,0:T(4,128)S(1)}, ...), condition=%wide.region_5.7_spmd, body=%wide.region_3.6_spmd.sunk | while | flops 9486662 | bytes 816557 | solution.py:141
  73.6 0.1 reshape.544
  73.7 0.6 gather_fusion.1
  74.3 0.1 fusion.65
  74.4 0.1 broadcast_and_fusion.2
  74.5 0.1 reshape.545
  74.6 0.6 gather_fusion.2
  75.3 9.3 %select_reduce_fusion.2 = f32[4,128]{1,0:T(4,128)S(1)} fusion(f32[4,8,128]{2,1,0:T(8,128)S(1)} %fusion.66, f32[4,128]{1,0:T(4,128)S(1)} %get-tuple-element.368, f32[4,8,128]{2,1,0:T(8,128)S(1)} %get-tuple-element.369, f32[4,128]{1,0:T(4,128)S(1)} %get-tuple-element.370, f32[4,8,128]{2,1,0:T(8,128)S(1)} %get-tuple-element.371, ...), kind=kLoop, calls=%fused_computation.63.clone.1 | loop fusion | flops 9436672 | bytes 96768 | tf_op jit(solution)/shard_map/while/body/eval_jaxpr/reduce_sum | solution.py:89
  84.6 0.1 reshape.544
  84.7 0.6 gather_fusion.1
  85.5 0.1 broadcast_and_fusion.2
  85.6 0.1 reshape.545
  85.7 0.6 gather_fusion.2
  86.4 9.3 %select_reduce_fusion.2 = f32[4,128]{1,0:T(4,128)S(1)} fusion(f32[4,8,128]{2,1,0:T(8,128)S(1)} %fusion.66, f32[4,128]{1,0:T(4,128)S(1)} %get-tuple-element.368, f32[4,8,128]{2,1,0:T(8,128)S(1)} %get-tuple-element.369, f32[4,128]{1,0:T(4,128)S(1)} %get-tuple-element.370, f32[4,8,128]{2,1,0:T(8,128)S(1)} %get-tuple-element.371, ...), kind=kLoop, calls=%fused_computation.63.clone.1 | loop fusion | flops 9436672 | bytes 96768 | tf_op jit(solution)/shard_map/while/body/eval_jaxpr/reduce_sum | solution.py:89
  95.7 0.1 reshape.544
  95.8 0.6 gather_fusion.1
  96.5 0.1 broadcast_and_fusion.2
  96.6 0.1 reshape.545
  96.7 0.6 gather_fusion.2
  97.4 9.3 %select_reduce_fusion.2 = f32[4,128]{1,0:T(4,128)S(1)} fusion(f32[4,8,128]{2,1,0:T(8,128)S(1)} %fusion.66, f32[4,128]{1,0:T(4,128)S(1)} %get-tuple-element.368, f32[4,8,128]{2,1,0:T(8,128)S(1)} %get-tuple-element.369, f32[4,128]{1,0:T(4,128)S(1)} %get-tuple-element.370, f32[4,8,128]{2,1,0:T(8,128)S(1)} %get-tuple-element.371, ...), kind=kLoop, calls=%fused_computation.63.clone.1 | loop fusion | flops 9436672 | bytes 96768 | tf_op jit(solution)/shard_map/while/body/eval_jaxpr/reduce_sum | solution.py:89
  106.7 0.1 reshape.544
  106.8 0.6 gather_fusion.1
  107.5 0.1 broadcast_and_fusion.2
  107.6 0.1 reshape.545
  107.7 0.6 gather_fusion.2
  108.4 9.3 %select_reduce_fusion.2 = f32[4,128]{1,0:T(4,128)S(1)} fusion(f32[4,8,128]{2,1,0:T(8,128)S(1)} %fusion.66, f32[4,128]{1,0:T(4,128)S(1)} %get-tuple-element.368, f32[4,8,128]{2,1,0:T(8,128)S(1)} %get-tuple-element.369, f32[4,128]{1,0:T(4,128)S(1)} %get-tuple-element.370, f32[4,8,128]{2,1,0:T(8,128)S(1)} %get-tuple-element.371, ...), kind=kLoop, calls=%fused_computation.63.clone.1 | loop fusion | flops 9436672 | bytes 96768 | tf_op jit(solution)/shard_map/while/body/eval_jaxpr/reduce_sum | solution.py:89
  117.7 0.6 reduce_sum.35
  118.3 6.6 %psum.28 = f32[]{:T(128)} all-reduce(f32[]{:T(128)} %reduce_sum.35), channel_id=1, replica_groups=mesh['slab_0'=4,'slab_1'=8,'slab_2'=4,'slab_3'=2] {'slab_0'}, use_global_device_ids=true, to_apply=%region_7.9 | all-reduce | flops 1 | bytes 8 | tf_op jit(solution)/shard_map/psum | solution.py:21
  124.9 12.9 %psum.29 = f32[]{:T(128)} all-reduce(f32[]{:T(128)} %psum.28), channel_id=1, replica_groups=mesh['slab_0'=4,'slab_1'=8,'slab_2'=4,'slab_3'=2] {'slab_1'}, use_global_device_ids=true, to_apply=%region_8.10 | all-reduce | flops 1 | bytes 8 | tf_op jit(solution)/shard_map/psum | solution.py:21
  137.9 12.6 %psum.30 = f32[]{:T(128)} all-reduce(f32[]{:T(128)} %psum.29), channel_id=1, replica_groups=mesh['slab_0'=4,'slab_1'=8,'slab_2'=4,'slab_3'=2] {'slab_2'}, use_global_device_ids=true, to_apply=%region_9.11 | all-reduce | flops 1 | bytes 8 | tf_op jit(solution)/shard_map/psum | solution.py:21
  150.5 13.3 %psum.31 = f32[]{:T(128)} all-reduce(f32[]{:T(128)} %psum.30), channel_id=1, replica_groups=mesh['slab_0'=4,'slab_1'=8,'slab_2'=4,'slab_3'=2] {'slab_3'}, use_global_device_ids=true, to_apply=%region_10.12 | all-reduce | flops 1 | bytes 8 | tf_op jit(solution)/shard_map/psum | solution.py:21
  (122 shorter events, 2.9 us)
Async XLA Ops:
  2.1 13.5 %collective-permute-start = (f32[7,2048]{1,0:T(8,128)S(1)}, f32[7,2048]{1,0:T(8,128)S(1)}, u32[]{:S(2)}, u32[]{:S(2)}) collective-permute-start(f32[7,2048]{1,0:T(8,128)S(1)} %concatenate.21), channel_id=1, source_target_pairs={{0,2},{1,3},{2,4},{3,5},{4,6},{5,7},{6,8},{7,9},{8,10},{9,11},{10,... | collective-permute-start | bytes 172040 | tf_op jit(solution)/shard_map/ppermute | solution.py:16
  4.3 11.3 %collective-permute-start.1 = (f32[7,2048]{1,0:T(8,128)S(1)}, f32[7,2048]{1,0:T(8,128)S(1)}, u32[]{:S(2)}, u32[]{:S(2)}) collective-permute-start(f32[7,2048]{1,0:T(8,128)S(1)} %concatenate.21), channel_id=1, source_target_pairs={{0,1},{1,2},{2,3},{3,4},{4,5},{5,6},{6,7},{7,8},{8,9},{9,10},{10,1... | collective-permute-start | bytes 172040 | tf_op jit(solution)/shard_map/ppermute | solution.py:16
  6.5 9.2 %collective-permute-start.2 = (f32[7,2048]{1,0:T(8,128)S(1)}, f32[7,2048]{1,0:T(8,128)S(1)}, u32[]{:S(2)}, u32[]{:S(2)}) collective-permute-start(f32[7,2048]{1,0:T(8,128)S(1)} %concatenate.21), channel_id=1, source_target_pairs={{0,255},{1,0},{2,1},{3,2},{4,3},{5,4},{6,5},{7,6},{8,7},{9,8},{10,... | collective-permute-start | bytes 172040 | tf_op jit(solution)/shard_map/ppermute | solution.py:16
  6.5 9.5 %collective-permute-start.3 = (f32[7,2048]{1,0:T(8,128)S(1)}, f32[7,2048]{1,0:T(8,128)S(1)}, u32[]{:S(2)}, u32[]{:S(2)}) collective-permute-start(f32[7,2048]{1,0:T(8,128)S(1)} %concatenate.21), channel_id=1, source_target_pairs={{0,254},{1,255},{2,0},{3,1},{4,2},{5,3},{6,4},{7,5},{8,6},{9,7},{1... | collective-permute-start | bytes 172040 | tf_op jit(solution)/shard_map/ppermute | solution.py:16
  63.1 9.7 %collective-permute-start.4 = (f32[2048]{0:T(1024)S(1)}, f32[2048]{0:T(1024)S(1)}, u32[]{:S(2)}, u32[]{:S(2)}) collective-permute-start(f32[2048]{0:T(1024)S(1)} %bitcast.192), channel_id=1, source_target_pairs={{0,2},{1,3},{2,4},{3,5},{4,6},{5,7},{6,8},{7,9},{8,10},{9,11},{10,... | collective-permute-start | bytes 24584 | tf_op jit(solution)/shard_map/ppermute | solution.py:16
  63.2 9.6 %collective-permute-start.5 = (f32[2048]{0:T(1024)S(1)}, f32[2048]{0:T(1024)S(1)}, u32[]{:S(2)}, u32[]{:S(2)}) collective-permute-start(f32[2048]{0:T(1024)S(1)} %bitcast.193), channel_id=1, source_target_pairs={{0,1},{1,2},{2,3},{3,4},{4,5},{5,6},{6,7},{7,8},{8,9},{9,10},{10,1... | collective-permute-start | bytes 24584 | tf_op jit(solution)/shard_map/ppermute | solution.py:16
  64.6 8.2 %collective-permute-start.6 = (f32[2048]{0:T(1024)S(1)}, f32[2048]{0:T(1024)S(1)}, u32[]{:S(2)}, u32[]{:S(2)}) collective-permute-start(f32[2048]{0:T(1024)S(1)} %bitcast.194), channel_id=1, source_target_pairs={{0,255},{1,0},{2,1},{3,2},{4,3},{5,4},{6,5},{7,6},{8,7},{9,8},{10,... | collective-permute-start | bytes 24584 | tf_op jit(solution)/shard_map/ppermute | solution.py:16
  65.4 8.2 %collective-permute-start.7 = (f32[2048]{0:T(1024)S(1)}, f32[2048]{0:T(1024)S(1)}, u32[]{:S(2)}, u32[]{:S(2)}) collective-permute-start(f32[2048]{0:T(1024)S(1)} %bitcast.195), channel_id=1, source_target_pairs={{0,254},{1,255},{2,0},{3,1},{4,2},{5,3},{6,4},{7,5},{8,6},{9,7},{1... | collective-permute-start | bytes 24584 | tf_op jit(solution)/shard_map/ppermute | solution.py:16
  117.7 46.2 %copy-start = (f32[4,4,128]{2,1,0:T(4,128)}, f32[4,4,128]{2,1,0:T(4,128)S(1)}, u32[]{:S(2)}) copy-start(f32[4,4,128]{2,1,0:T(4,128)S(1)} %get-tuple-element.470) | copy-start | bytes 24580
  117.7 46.1 %copy-start.1 = (f32[4,4,128]{2,1,0:T(4,128)}, f32[4,4,128]{2,1,0:T(4,128)S(1)}, u32[]{:S(2)}) copy-start(f32[4,4,128]{2,1,0:T(4,128)S(1)} %get-tuple-element.156) | copy-start | bytes 24580
where the time goes:
time: 164 us
  other arithmetic  82.8 us (50%)
  blocking collectives  45.5 us (28%)
  starting transfers between devices  21.7 us (13%)
  local copies, waits for them, and re-layouts  10.9 us (7%)
    psum x4, blocking collectives, by_axis(): shard = lax.psum(shard, axis)  45.5 us
    reduce_sum x4, other arithmetic, born_block(): integral = jnp.sum(jnp.where(counted, pair_term, 0.0), axis=(2, 3))  41.8 us
    reduce_sum x4, other arithmetic, energy_block(): result = -0.5 * own_atoms[3] * jnp.sum(pair_term, axis=(2, 3))  37 us
    ppermute x8, starting transfers between devices, passed_along(): return lax.ppermute(value, axis, pairs)  21.7 us
    gather x8, local copies, waits for them, and re-layouts, one_block(): partner_atoms = jnp.take(tiled, list_block, axis=1)  4.68 us
  transfers between devices with their start and end apart: 8, of which 2 were waited for; matrix products, arithmetic and copies ran while one was open for 1% of the time, Pallas kernels for 0%

commit v1 on v0

--- a/solution.py
+++ b/solution.py
@@ -18,7 +18,7 @@
 
 def by_axis(shard, axes):
     for axis in axes:
-        shard = lax.psum(shard, axis)
+        shard = jnp.sum(lax.all_gather(shard, axis), 0)
     return shard
 
 

time: 164 us -> 173 us (1.055)
  local copies, waits for them, and re-layouts: 10.9 us -> 19.3 us
  other arithmetic: 82.8 us -> 85.2 us
  blocking collectives: 45.5 us -> 43.1 us
    psum x4 -> x0, blocking collectives: 45.5 us -> none  [by_axis(): shard = lax.psum(shard, axis)]
    unnamed x0 -> x4, blocking collectives: none -> 43.1 us
    unnamed x13 -> x33, local copies, waits for them, and re-layouts: 0.81 us -> 9.26 us
    reduce_sum x0 -> x4, other arithmetic: none -> 2.41 us  [by_axis(): shard = jnp.sum(lax.all_gather(shard, axis), 0)]
where the time goes in v1:
time: 173 us; the launch traced here: 172 us
  other arithmetic  85.2 us (49%)
  blocking collectives  43.1 us (25%)
  starting transfers between devices  21.5 us (12%)
  local copies, waits for them, and re-layouts  19.3 us (11%)
    unnamed x4, blocking collectives  43.1 us
    reduce_sum x4, other arithmetic, born_block(): integral = jnp.sum(jnp.where(counted, pair_term, 0.0), axis=(2, 3))  41.8 us
    reduce_sum x4, other arithmetic, energy_block(): result = -0.5 * own_atoms[3] * jnp.sum(pair_term, axis=(2, 3))  37 us
    ppermute x8, starting transfers between devices, passed_along(): return lax.ppermute(value, axis, pairs)  21.5 us
    unnamed x33, local copies, waits for them, and re-layouts  9.26 us
    gather x8, local copies, waits for them, and re-layouts, one_block(): partner_atoms = jnp.take(tiled, list_block, axis=1)  4.68 us
  transfers between devices with their start and end apart: 8, of which 2 were waited for; matrix products, arithmetic and copies ran while one was open for 1% of the time, Pallas kernels for 0%

profile of v1, /device:TPU:1, one launch (start us, length us, event | category | flops | bytes accessed | tf_op | source)
XLA Modules:
  0.0 172.2 jit_solution(17859064888641332485)
XLA Ops:
  1.3 0.8 concatenate.21
  2.1 2.2 %collective-permute-start = (f32[7,2048]{1,0:T(8,128)S(1)}, f32[7,2048]{1,0:T(8,128)S(1)}, u32[]{:S(2)}, u32[]{:S(2)}) collective-permute-start(f32[7,2048]{1,0:T(8,128)S(1)} %concatenate.21), channel_id=1, source_target_pairs={{0,2},{1,3},{2,4},{3,5},{4,6},{5,7},{6,8},{7,9},{8,10},{9,11},{10,... | collective-permute-start | bytes 172040 | tf_op jit(solution)/shard_map/ppermute | solution.py:16
  4.3 2.1 %collective-permute-start.1 = (f32[7,2048]{1,0:T(8,128)S(1)}, f32[7,2048]{1,0:T(8,128)S(1)}, u32[]{:S(2)}, u32[]{:S(2)}) collective-permute-start(f32[7,2048]{1,0:T(8,128)S(1)} %concatenate.21), channel_id=1, source_target_pairs={{0,1},{1,2},{2,3},{3,4},{4,5},{5,6},{6,7},{7,8},{8,9},{9,10},{10,1... | collective-permute-start | bytes 172040 | tf_op jit(solution)/shard_map/ppermute | solution.py:16
  6.5 7.6 %collective-permute-start.3 = (f32[7,2048]{1,0:T(8,128)S(1)}, f32[7,2048]{1,0:T(8,128)S(1)}, u32[]{:S(2)}, u32[]{:S(2)}) collective-permute-start(f32[7,2048]{1,0:T(8,128)S(1)} %concatenate.21), channel_id=1, source_target_pairs={{0,254},{1,255},{2,0},{3,1},{4,2},{5,3},{6,4},{7,5},{8,6},{9,7},{1... | collective-permute-start | bytes 172040 | tf_op jit(solution)/shard_map/ppermute | solution.py:16
  14.1 0.8 copy.25
  14.9 0.7 reshape.487
  15.7 0.3 collective-permute-done.3
  16.1 47.0 %while.23 = (s32[]{:T(128)}, f32[4,4,128]{2,1,0:T(4,128)S(1)}, f32[4,7,4,128]{3,2,1,0:T(4,128)S(1)}, s32[4,4]{1,0:T(4,128)S(1)}, s32[4,4,8]{2,1,0:T(4,128)S(1)},...) while((s32[]{:T(128)}, f32[4,4,128]{2,1,0:T(4,128)S(1)}, ...), condition=%wide.region_2.4_spmd, body=%wide.region_0.3_spmd.sunk | while | flops 23141128 | bytes 918585 | solution.py:117
  16.1 0.1 reshape.559
  16.2 0.6 gather_fusion
  16.8 0.1 select_bitcast_fusion.2
  17.4 10.4 %fusion.63 = f32[4,128]{1,0:T(4,128)S(1)} fusion(f32[4,128]{1,0:T(4,128)S(1)} %get-tuple-element.337, f32[4,8,128]{2,1,0:T(8,128)S(1)} %get-tuple-element.345, f32[4,8,128]{2,1,0:T(8,128)S(1)} %get-tuple-element.346, f32[4,8,128]{2,1,0:T(8,128)S(1)} %bitcast.196, f32[4,128]{1,0:T(4,128)S(1)} %get-tuple-element.348, f32[4,8,128]{2,1,0:T(8,128)S(1)} %bitcast.197, ...), kind=kLoop, calls=%fused_computation.16.clone.1 | loop fusion | flops 23068160 | bytes 117248 | tf_op jit(solution)/shard_map/while/body/eval_jaxpr/reduce_sum | solution.py:67
  27.9 0.1 reshape.559
  28.0 0.6 gather_fusion
  28.6 0.1 select_bitcast_fusion.2
  29.1 10.4 %fusion.63 = f32[4,128]{1,0:T(4,128)S(1)} fusion(f32[4,128]{1,0:T(4,128)S(1)} %get-tuple-element.337, f32[4,8,128]{2,1,0:T(8,128)S(1)} %get-tuple-element.345, f32[4,8,128]{2,1,0:T(8,128)S(1)} %get-tuple-element.346, f32[4,8,128]{2,1,0:T(8,128)S(1)} %bitcast.196, f32[4,128]{1,0:T(4,128)S(1)} %get-tuple-element.348, f32[4,8,128]{2,1,0:T(8,128)S(1)} %bitcast.197, ...), kind=kLoop, calls=%fused_computation.16.clone.1 | loop fusion | flops 23068160 | bytes 117248 | tf_op jit(solution)/shard_map/while/body/eval_jaxpr/reduce_sum | solution.py:67
  39.6 0.1 reshape.559
  39.7 0.6 gather_fusion
  40.3 0.1 select_bitcast_fusion.2
  40.9 10.4 %fusion.63 = f32[4,128]{1,0:T(4,128)S(1)} fusion(f32[4,128]{1,0:T(4,128)S(1)} %get-tuple-element.337, f32[4,8,128]{2,1,0:T(8,128)S(1)} %get-tuple-element.345, f32[4,8,128]{2,1,0:T(8,128)S(1)} %get-tuple-element.346, f32[4,8,128]{2,1,0:T(8,128)S(1)} %bitcast.196, f32[4,128]{1,0:T(4,128)S(1)} %get-tuple-element.348, f32[4,8,128]{2,1,0:T(8,128)S(1)} %bitcast.197, ...), kind=kLoop, calls=%fused_computation.16.clone.1 | loop fusion | flops 23068160 | bytes 117248 | tf_op jit(solution)/shard_map/while/body/eval_jaxpr/reduce_sum | solution.py:67
  51.4 0.1 reshape.559
  51.5 0.6 gather_fusion
  52.1 0.1 select_bitcast_fusion.2
  52.6 10.4 %fusion.63 = f32[4,128]{1,0:T(4,128)S(1)} fusion(f32[4,128]{1,0:T(4,128)S(1)} %get-tuple-element.337, f32[4,8,128]{2,1,0:T(8,128)S(1)} %get-tuple-element.345, f32[4,8,128]{2,1,0:T(8,128)S(1)} %get-tuple-element.346, f32[4,8,128]{2,1,0:T(8,128)S(1)} %bitcast.196, f32[4,128]{1,0:T(4,128)S(1)} %get-tuple-element.348, f32[4,8,128]{2,1,0:T(8,128)S(1)} %bitcast.197, ...), kind=kLoop, calls=%fused_computation.16.clone.1 | loop fusion | flops 23068160 | bytes 117248 | tf_op jit(solution)/shard_map/while/body/eval_jaxpr/reduce_sum | solution.py:67
  63.1 0.1 collective-permute-start.4
  63.2 0.7 dynamic-slice
  63.9 1.3 collective-permute-start.5
  65.2 0.7 collective-permute-start.6
  65.9 7.4 %collective-permute-start.7 = (f32[2048]{0:T(1024)S(1)}, f32[2048]{0:T(1024)S(1)}, u32[]{:S(2)}, u32[]{:S(2)}) collective-permute-start(f32[2048]{0:T(1024)S(1)} %bitcast.203), channel_id=1, source_target_pairs={{0,254},{1,255},{2,0},{3,1},{4,2},{5,3},{6,4},{7,5},{8,6},{9,7},{1... | collective-permute-start | bytes 24584 | tf_op jit(solution)/shard_map/ppermute | solution.py:16
  73.4 0.7 collective-permute-done.7
  74.1 44.1 %while.24 = (s32[]{:T(128)}, f32[4,4,128]{2,1,0:T(4,128)S(1)}, f32[4,7,4,128]{3,2,1,0:T(4,128)S(1)}, s32[4,4]{1,0:T(4,128)S(1)}, s32[4,4,8]{2,1,0:T(4,128)S(1)},...) while((s32[]{:T(128)}, f32[4,4,128]{2,1,0:T(4,128)S(1)}, ...), condition=%wide.region_5.7_spmd, body=%wide.region_3.6_spmd.sunk | while | flops 9486662 | bytes 816557 | solution.py:141
  74.2 0.1 reshape.564
  74.2 0.6 gather_fusion.1
  75.1 0.1 reshape.565
  75.2 0.6 gather_fusion.2
  75.9 9.3 %select_reduce_fusion.2 = f32[4,128]{1,0:T(4,128)S(1)} fusion(f32[4,8,128]{2,1,0:T(8,128)S(1)} %fusion.66, f32[4,128]{1,0:T(4,128)S(1)} %get-tuple-element.368, f32[4,8,128]{2,1,0:T(8,128)S(1)} %get-tuple-element.369, f32[4,128]{1,0:T(4,128)S(1)} %get-tuple-element.370, f32[4,8,128]{2,1,0:T(8,128)S(1)} %get-tuple-element.371, ...), kind=kLoop, calls=%fused_computation.63.clone.1 | loop fusion | flops 9436672 | bytes 96768 | tf_op jit(solution)/shard_map/while/body/eval_jaxpr/reduce_sum | solution.py:89
  85.3 0.6 gather_fusion.1
  86.1 0.1 reshape.565
  86.2 0.6 gather_fusion.2
  86.9 9.3 %select_reduce_fusion.2 = f32[4,128]{1,0:T(4,128)S(1)} fusion(f32[4,8,128]{2,1,0:T(8,128)S(1)} %fusion.66, f32[4,128]{1,0:T(4,128)S(1)} %get-tuple-element.368, f32[4,8,128]{2,1,0:T(8,128)S(1)} %get-tuple-element.369, f32[4,128]{1,0:T(4,128)S(1)} %get-tuple-element.370, f32[4,8,128]{2,1,0:T(8,128)S(1)} %get-tuple-element.371, ...), kind=kLoop, calls=%fused_computation.63.clone.1 | loop fusion | flops 9436672 | bytes 96768 | tf_op jit(solution)/shard_map/while/body/eval_jaxpr/reduce_sum | solution.py:89
  96.3 0.6 gather_fusion.1
  97.2 0.1 reshape.565
  97.3 0.6 gather_fusion.2
  98.0 9.3 %select_reduce_fusion.2 = f32[4,128]{1,0:T(4,128)S(1)} fusion(f32[4,8,128]{2,1,0:T(8,128)S(1)} %fusion.66, f32[4,128]{1,0:T(4,128)S(1)} %get-tuple-element.368, f32[4,8,128]{2,1,0:T(8,128)S(1)} %get-tuple-element.369, f32[4,128]{1,0:T(4,128)S(1)} %get-tuple-element.370, f32[4,8,128]{2,1,0:T(8,128)S(1)} %get-tuple-element.371, ...), kind=kLoop, calls=%fused_computation.63.clone.1 | loop fusion | flops 9436672 | bytes 96768 | tf_op jit(solution)/shard_map/while/body/eval_jaxpr/reduce_sum | solution.py:89
  107.4 0.6 gather_fusion.1
  108.2 0.1 reshape.565
  108.3 0.6 gather_fusion.2
  109.0 9.3 %select_reduce_fusion.2 = f32[4,128]{1,0:T(4,128)S(1)} fusion(f32[4,8,128]{2,1,0:T(8,128)S(1)} %fusion.66, f32[4,128]{1,0:T(4,128)S(1)} %get-tuple-element.368, f32[4,8,128]{2,1,0:T(8,128)S(1)} %get-tuple-element.369, f32[4,128]{1,0:T(4,128)S(1)} %get-tuple-element.370, f32[4,8,128]{2,1,0:T(8,128)S(1)} %get-tuple-element.371, ...), kind=kLoop, calls=%fused_computation.63.clone.1 | loop fusion | flops 9436672 | bytes 96768 | tf_op jit(solution)/shard_map/while/body/eval_jaxpr/reduce_sum | solution.py:89
  118.3 0.6 reduce_sum.71
  118.9 1.4 dynamic-update-slice
  120.3 0.7 dynamic-slice.1
  121.0 6.0 %all-reduce = f32[4]{0:T(128)S(1)} all-reduce(f32[4]{0:T(128)S(1)} %dynamic-update-slice), channel_id=1, replica_groups=mesh['slab_0'=4,'slab_1'=8,'slab_2'=4,'slab_3'=2] {'slab_0'}, use_global_device_ids=true, to_apply=%add | all-reduce | flops 4 | bytes 32
  127.0 0.6 reduce_sum.72
  127.6 1.4 dynamic-update-slice.1
  129.0 0.7 dynamic-slice.2
  129.7 12.5 %all-reduce.1 = f32[8]{0:T(128)S(1)} all-reduce(f32[8]{0:T(128)S(1)} %dynamic-update-slice.1), channel_id=1, replica_groups=mesh['slab_0'=4,'slab_1'=8,'slab_2'=4,'slab_3'=2] {'slab_1'}, use_global_device_ids=true, to_apply=%add.1 | all-reduce | flops 8 | bytes 64
  142.2 0.6 reduce_sum.73
  142.8 1.4 dynamic-update-slice.2
  144.2 0.7 dynamic-slice.3
  144.9 11.9 %all-reduce.2 = f32[4]{0:T(128)S(1)} all-reduce(f32[4]{0:T(128)S(1)} %dynamic-update-slice.2), channel_id=1, replica_groups=mesh['slab_0'=4,'slab_1'=8,'slab_2'=4,'slab_3'=2] {'slab_2'}, use_global_device_ids=true, to_apply=%add.2 | all-reduce | flops 4 | bytes 32
  156.8 0.6 reduce_sum.74
  157.4 1.4 dynamic-update-slice.3
  158.9 12.7 %all-reduce.3 = f32[2]{0:T(128)S(1)} all-reduce(f32[2]{0:T(128)S(1)} %dynamic-update-slice.3), channel_id=1, replica_groups=mesh['slab_0'=4,'slab_1'=8,'slab_2'=4,'slab_3'=2] {'slab_3'}, use_global_device_ids=true, to_apply=%add.3 | all-reduce | flops 2 | bytes 16
  171.6 0.6 reduce_sum.75
  (146 shorter events, 3.9 us)
Async XLA Ops:
  2.1 13.5 %collective-permute-start = (f32[7,2048]{1,0:T(8,128)S(1)}, f32[7,2048]{1,0:T(8,128)S(1)}, u32[]{:S(2)}, u32[]{:S(2)}) collective-permute-start(f32[7,2048]{1,0:T(8,128)S(1)} %concatenate.21), channel_id=1, source_target_pairs={{0,2},{1,3},{2,4},{3,5},{4,6},{5,7},{6,8},{7,9},{8,10},{9,11},{10,... | collective-permute-start | bytes 172040 | tf_op jit(solution)/shard_map/ppermute | solution.py:16
  4.3 11.3 %collective-permute-start.1 = (f32[7,2048]{1,0:T(8,128)S(1)}, f32[7,2048]{1,0:T(8,128)S(1)}, u32[]{:S(2)}, u32[]{:S(2)}) collective-permute-start(f32[7,2048]{1,0:T(8,128)S(1)} %concatenate.21), channel_id=1, source_target_pairs={{0,1},{1,2},{2,3},{3,4},{4,5},{5,6},{6,7},{7,8},{8,9},{9,10},{10,1... | collective-permute-start | bytes 172040 | tf_op jit(solution)/shard_map/ppermute | solution.py:16
  6.5 9.2 %collective-permute-start.2 = (f32[7,2048]{1,0:T(8,128)S(1)}, f32[7,2048]{1,0:T(8,128)S(1)}, u32[]{:S(2)}, u32[]{:S(2)}) collective-permute-start(f32[7,2048]{1,0:T(8,128)S(1)} %concatenate.21), channel_id=1, source_target_pairs={{0,255},{1,0},{2,1},{3,2},{4,3},{5,4},{6,5},{7,6},{8,7},{9,8},{10,... | collective-permute-start | bytes 172040 | tf_op jit(solution)/shard_map/ppermute | solution.py:16
  6.5 9.5 %collective-permute-start.3 = (f32[7,2048]{1,0:T(8,128)S(1)}, f32[7,2048]{1,0:T(8,128)S(1)}, u32[]{:S(2)}, u32[]{:S(2)}) collective-permute-start(f32[7,2048]{1,0:T(8,128)S(1)} %concatenate.21), channel_id=1, source_target_pairs={{0,254},{1,255},{2,0},{3,1},{4,2},{5,3},{6,4},{7,5},{8,6},{9,7},{1... | collective-permute-start | bytes 172040 | tf_op jit(solution)/shard_map/ppermute | solution.py:16
  16.1 47.1 %copy-start.5 = (u32[256]{0:T(256)S(1)}, u32[256]{0:T(256)}, u32[]{:S(2)}) copy-start(u32[256]{0:T(256)} %constant.154) | copy-start | bytes 3076
  63.1 10.2 %collective-permute-start.4 = (f32[2048]{0:T(1024)S(1)}, f32[2048]{0:T(1024)S(1)}, u32[]{:S(2)}, u32[]{:S(2)}) collective-permute-start(f32[2048]{0:T(1024)S(1)} %bitcast.200), channel_id=1, source_target_pairs={{0,2},{1,3},{2,4},{3,5},{4,6},{5,7},{6,8},{7,9},{8,10},{9,11},{10,... | collective-permute-start | bytes 24584 | tf_op jit(solution)/shard_map/ppermute | solution.py:16
  63.9 9.5 %collective-permute-start.5 = (f32[2048]{0:T(1024)S(1)}, f32[2048]{0:T(1024)S(1)}, u32[]{:S(2)}, u32[]{:S(2)}) collective-permute-start(f32[2048]{0:T(1024)S(1)} %bitcast.201), channel_id=1, source_target_pairs={{0,1},{1,2},{2,3},{3,4},{4,5},{5,6},{6,7},{7,8},{8,9},{9,10},{10,1... | collective-permute-start | bytes 24584 | tf_op jit(solution)/shard_map/ppermute | solution.py:16
  65.2 8.1 %collective-permute-start.6 = (f32[2048]{0:T(1024)S(1)}, f32[2048]{0:T(1024)S(1)}, u32[]{:S(2)}, u32[]{:S(2)}) collective-permute-start(f32[2048]{0:T(1024)S(1)} %bitcast.202), channel_id=1, source_target_pairs={{0,255},{1,0},{2,1},{3,2},{4,3},{5,4},{6,5},{7,6},{8,7},{9,8},{10,... | collective-permute-start | bytes 24584 | tf_op jit(solution)/shard_map/ppermute | solution.py:16
  65.9 8.2 %collective-permute-start.7 = (f32[2048]{0:T(1024)S(1)}, f32[2048]{0:T(1024)S(1)}, u32[]{:S(2)}, u32[]{:S(2)}) collective-permute-start(f32[2048]{0:T(1024)S(1)} %bitcast.203), channel_id=1, source_target_pairs={{0,254},{1,255},{2,0},{3,1},{4,2},{5,3},{6,4},{7,5},{8,6},{9,7},{1... | collective-permute-start | bytes 24584 | tf_op jit(solution)/shard_map/ppermute | solution.py:16
  74.1 46.2 %copy-start.4 = (u32[256]{0:T(256)S(1)}, u32[256]{0:T(256)}, u32[]{:S(2)}) copy-start(u32[256]{0:T(256)} %constant.159) | copy-start | bytes 3076
  74.1 54.9 %copy-start.3 = (u32[256]{0:T(256)S(1)}, u32[256]{0:T(256)}, u32[]{:S(2)}) copy-start(u32[256]{0:T(256)} %constant.164) | copy-start | bytes 3076
  74.1 70.1 %copy-start.2 = (u32[256]{0:T(256)S(1)}, u32[256]{0:T(256)}, u32[]{:S(2)}) copy-start(u32[256]{0:T(256)} %constant.169) | copy-start | bytes 3076
  118.3 53.9 %copy-start = (f32[4,4,128]{2,1,0:T(4,128)}, f32[4,4,128]{2,1,0:T(4,128)S(1)}, u32[]{:S(2)}) copy-start(f32[4,4,128]{2,1,0:T(4,128)S(1)} %get-tuple-element.470) | copy-start | bytes 24580
  118.3 53.9 %copy-start.1 = (f32[4,4,128]{2,1,0:T(4,128)}, f32[4,4,128]{2,1,0:T(4,128)S(1)}, u32[]{:S(2)}) copy-start(f32[4,4,128]{2,1,0:T(4,128)S(1)} %get-tuple-element.156) | copy-start | bytes 24580
